TPU v7x, 128 devices: a whole 4x4x4 slice. The times are simulated.
128 devices in a mesh: dp: 64 (over y, z_lo, x, core), rep: 2 (over z_hi).
Axes of the slice: x: 4, y: 4, z: 4 (z_hi: 2, z_lo: 2; z = z_hi * 2 + z_lo), core: 2. Of those that a mesh axis runs over, the one named last changes fastest.
Arguments:
- queries: bfloat16 [8192, 2048], P(('dp', 'rep')), may hold values from -24 to 24
- documents: bfloat16 [8192, 2048], P(('dp', 'rep')), may hold values from -24 to 24
- partner: int32 [8192], P(('dp', 'rep')), may hold values from 0 to 8191, each once
Outputs:
- grad_queries: float32 [8192, 2048], P(('dp', 'rep'))
- grad_documents: float32 [8192, 2048], P(('dp', 'rep'))
Inputs may be any that keep to these rules, and one draw needn't show every extreme that they name: `partner`: every document index appears exactly once.
All inputs are finite; a program needn't handle non-finite values.
Results may differ from a plain program's by a relative error of at most 0.0031.
Values may be sent and summed in bfloat16 or wider, within the bound.
A program may use at most 256 MiB of HBM per device.

v0:
```python
import jax
import jax.numpy as jnp
from jax import lax
from jax.sharding import Mesh
from jax.sharding import PartitionSpec as P

WIDTHS = 9
DP = ("dp_0", "dp_1", "dp_2", "dp_3")
DP_REP = ("dp_0", "dp_1", "dp_2", "dp_3", "rep")
logit_gain = 3.0


def laid_out(blocks, dim):
    blocks = jnp.moveaxis(blocks, 0, dim)
    shape = blocks.shape
    return blocks.reshape(*shape[:dim], shape[dim] * shape[dim + 1], *shape[dim + 2 :])


def copy_for_each(x, axis):
    copies = jnp.broadcast_to(x, (lax.axis_size(axis), *x.shape))
    return lax.all_to_all(copies, axis, split_axis=0, concat_axis=0, tiled=True)


def collect(x, axis, dim):
    return laid_out(copy_for_each(x, axis), dim)


def collected_together(x, axis):
    leaves = jax.tree.leaves(x)
    turns = sorted(range(len(leaves)), key=lambda k: -leaves[k].size)
    width = (1, *leaves[turns[0]].shape)[-1]
    lines = [
        jnp.pad(leaves[k].reshape(-1), (0, -leaves[k].size % width)).reshape(-1, width)
        for k in turns
    ]
    both, at, found = (copy_for_each(jnp.concatenate(lines), axis), 0, {})
    for k, line in zip(turns, lines):
        piece = both[:, at : at + len(line)].reshape(len(both), -1)
        found[k] = piece[:, : leaves[k].size].reshape(-1, *leaves[k].shape)
        at += len(line)
    numbers = iter(range(len(leaves)))
    return jax.tree.map(lambda _: found[next(numbers)], x)


def folded_in_pairs(pieces, combine):
    while len(jax.tree.leaves(pieces)[0]) > 1:
        pieces = jax.vmap(combine)(
            *(jax.tree.map(lambda part: part[side::2], pieces) for side in (0, 1))
        )
    return jax.tree.map(lambda part: part[0], pieces)


def merged(x, axis, combine):
    pieces = collected_together(x, axis)
    return folded_in_pairs(pieces, combine)


def cut_along(x, dim, size):
    shape = x.shape
    blocks = x.reshape(*shape[:dim], size, shape[dim] // size, *shape[dim + 1 :])
    return jnp.moveaxis(blocks, dim, 0)


def sum_at_owner(x, axis, dim):
    blocks = cut_along(x, dim, lax.axis_size(axis))
    arrived = lax.all_to_all(blocks, axis, split_axis=0, concat_axis=0, tiled=True)
    return arrived.sum(axis=0)


def sum_by_chip(x, chips, core, dim):
    sizes = (lax.axis_size(chips), lax.axis_size(core))
    blocks = cut_along(x, dim, sizes[0] * sizes[1])
    inside = blocks.shape[1:]
    blocks = blocks.reshape(*sizes, *inside).swapaxes(0, 1).reshape(-1, *inside)
    blocks = lax.psum_scatter(blocks, core, scatter_dimension=0, tiled=True)
    return lax.psum_scatter(blocks, chips, scatter_dimension=0, tiled=True)[0]


def contract(first_op, second_op):
    return lax.dot_general(
        first_op, second_op, (((1,), (1,)), ((), ())), preferred_element_type=jnp.float32
    )


def width_list(feature_dim):
    return [feature_dim >> WIDTHS - 1 - nested for nested in range(WIDTHS)]


def scores(first_op, second_op):
    uppers = width_list(first_op.shape[1])
    result = []
    running = jnp.zeros((first_op.shape[0], second_op.shape[0]), jnp.float32)
    lower_col = 0
    for upper_col in uppers:
        running = running + contract(
            first_op[:, lower_col:upper_col], second_op[:, lower_col:upper_col]
        )
        result.append(running * (logit_gain * upper_col ** (-0.5)))
        lower_col = upper_col
    return result


def band_sums(logit_list, total_list, target, uppers):
    bands = [None] * len(uppers)
    running = None
    for nested in reversed(range(len(uppers))):
        scale = logit_gain * uppers[nested] ** (-0.5)
        weight = (jnp.exp(logit_list[nested] - total_list[nested]) - target) * scale
        running = weight if running is None else running + weight
        bands[nested] = running.astype(jnp.bfloat16)
    return bands


def spread(bands, operand, uppers, transposed):
    pieces = []
    lower_col = 0
    for nested, upper_col in enumerate(uppers):
        block_part = operand[:, lower_col:upper_col]
        if transposed:
            product = lax.dot_general(
                bands[nested],
                block_part,
                (((0,), (0,)), ((), ())),
                preferred_element_type=jnp.float32,
            )
        else:
            product = jnp.dot(bands[nested], block_part, preferred_element_type=jnp.float32)
        pieces.append(product)
        lower_col = upper_col
    return jnp.concatenate(pieces, axis=1)


def combine(first_pair, second_pair):
    biggest = jnp.maximum(first_pair[0], second_pair[0])
    return (
        biggest,
        first_pair[1] * jnp.exp(first_pair[0] - biggest)
        + second_pair[1] * jnp.exp(second_pair[0] - biggest),
    )


def on_device(queries, documents, partner):
    own_rows = queries.shape[0]
    uppers = width_list(queries.shape[1])
    rep_index = lax.axis_index("rep")
    rep_count = lax.axis_size("rep")
    pair_rows, pair_partner = (collect(queries, "rep", 0), collect(partner, "rep", 0))
    partner_docs = lax.all_gather(documents, DP, axis=0, tiled=True)
    col_pos = jnp.arange(partner_docs.shape[0], dtype=jnp.int32)
    col_ids = (col_pos // own_rows * rep_count + rep_index) * own_rows + col_pos % own_rows
    target = (pair_partner[:, None] == col_ids[None, :]).astype(jnp.float32)
    logit_list = scores(pair_rows, partner_docs)
    row_peaks = jnp.stack([jnp.max(logits, axis=1) for logits in logit_list])
    masses = jnp.stack(
        [
            jnp.sum(jnp.exp(logits - row_peaks[nested][:, None]), axis=1)
            for nested, logits in enumerate(logit_list)
        ]
    )
    row_peaks, masses = merged((row_peaks, masses), "rep", combine)
    totals = row_peaks + jnp.log(masses)
    bands = band_sums(
        logit_list, [totals[nested][:, None] for nested in range(len(uppers))], target, uppers
    )
    partial_queries = spread(bands, partner_docs, uppers, False)
    grad_queries = sum_at_owner(partial_queries, "rep", 0)
    sliced = [factor for factor in bands]
    grad_documents = sum_by_chip(
        spread(sliced, pair_rows, uppers, True), ("dp_0", "dp_1", "dp_2"), "dp_3", 0
    )
    return (grad_queries, grad_documents)


def solution(mesh):
    finer = Mesh(
        mesh.devices.reshape(4, 2, 4, 2, mesh.shape["rep"]), ("dp_0", "dp_1", "dp_2", "dp_3", "rep")
    )
    placed = (P(DP_REP, None), P(DP_REP, None), P(DP_REP))
    return jax.shard_map(
        on_device,
        mesh=finer,
        in_specs=placed,
        out_specs=(P(DP_REP, None), P(DP_REP, None)),
        check_vma=False,
    )
```

profile of v0, /device:TPU:0, one launch (start us, length us, event | category | flops | bytes accessed | tf_op | source)
XLA Modules:
  0.0 521.3 jit_solution(7170143682551162871)
XLA Ops:
  7.2 0.7 all-gather.2.cloned.1.call-update
  7.9 1.8 broadcast_in_dim.10
  9.7 5.3 %all-to-all-start = ((bf16[2,64,2048]{2,1,0:T(8,128)(2,1)}), bf16[2,64,2048]{2,1,0:T(8,128)(2,1)S(1)}, u32[]{:S(2)}, u32[]{:S(2)}) async-start(bf16[2,64,2048]{2,1,0:T(8,128)(2,1)} %broadcast_in_dim.10), calls=%async_computation | async-start | bytes 1048576 | tf_op jit(solution)/shard_map/all_to_all | solution.py:21
  15.0 9.5 %all-to-all-done = bf16[2,64,2048]{2,1,0:T(8,128)(2,1)S(1)} async-done(((bf16[2,64,2048]{2,1,0:T(8,128)(2,1)}), bf16[2,64,2048]{2,1,0:T(8,128)(2,1)S(1)}, u32[]{:S(2)}, u32[]{:S(2)}) %all-to-all-start) | async-done | bytes 524320 | tf_op jit(solution)/shard_map/all_to_all | solution.py:21
  24.4 0.6 broadcast_in_dim.12
  25.0 3.2 all-to-all-start.2
  28.2 105.5 %all-gather.2.cloned.1.call-done = bf16[4096,2048]{1,0:T(8,128)(2,1)} async-done(((bf16[64,2048]{1,0:T(8,128)(2,1)}), bf16[4096,2048]{1,0:T(8,128)(2,1)}) %all-gather.2.cloned.1.call-update) | async-done | bytes 16777232 | tf_op jit(solution)/shard_map/all_gather | solution.py:148
  133.7 1.7 multiply_reduce_fusion.7
  136.0 2.1 multiply_reduce_fusion.6
  138.6 2.1 multiply_reduce_fusion.5
  140.7 0.5 exponential_reduce_fusion.6
  141.2 2.1 multiply_reduce_fusion.4
  143.9 2.1 multiply_reduce_fusion.3
  146.5 2.0 multiply_reduce_fusion.2
  149.0 2.5 multiply_reduce_fusion.1
  152.0 4.1 multiply_reduce_fusion
  156.6 5.7 %fusion.110 = (f32[128]{0:T(128)S(1)}, f32[128,4096]{1,0:T(8,128)S(1)}) fusion(f32[128,4096]{1,0:T(8,128)S(1)} %get-tuple-element.34, bf16[4096,2048]{1,0:T(8,128)(2,1)} %all-gather.2.cloned.1.call-done, bf16[128,2048]{1,0:T(8,128)(2,1)} %bitcast.69), kind=kOutput, calls=%fused_computation.155 | convolution fusion | flops 1075314560 | bytes 12845568 | tf_op jit(solution)/shard_map/dot_general | solution.py:80
  162.3 1.3 copy-done.6
  164.1 0.6 broadcast_in_dim.11
  164.7 4.5 all-to-all-start.1
  169.2 0.5 broadcast.142
  169.8 0.6 reduce.3
  170.4 4.2 all-to-all-done.1
  174.7 8.6 %fusion.30 = (bf16[128,4096]{1,0:T(8,128)(2,1)S(1)}, bf16[128,4096]{1,0:T(8,128)(2,1)S(1)}, bf16[128,4096]{1,0:T(8,128)(2,1)S(1)}, bf16[128,4096]{1,0:T(8,128)(2...) fusion(f32[128,4096]{1,0:T(8,128)} %copy-done, ...), kind=kLoop, calls=%fused_computation.51 | loop fusion | flops 27787264 | bytes 27284480 | tf_op jit(solution)/shard_map/convert_element_type | solution.py:110
  183.4 1.3 convolution_dynamic-update-slice_fusion.8
  184.7 1.6 convolution_dynamic-update-slice_fusion.7
  186.3 1.1 convolution_dynamic-update-slice_fusion.6
  187.3 1.2 convolution_dynamic-update-slice_fusion.5
  188.5 1.4 convolution_dynamic-update-slice_fusion.4
  190.0 1.8 convolution_dynamic-update-slice_fusion.3
  191.8 2.7 convolution_dynamic-update-slice_fusion.2
  194.5 4.5 convolution_dynamic-update-slice_fusion.1
  199.0 8.2 %convolution_dynamic-update-slice_fusion = f32[4096,2048]{0,1:T(8,128)} fusion(f32[4096,2048]{0,1:T(8,128)} %convolution_dynamic-update-slice_fusion.1, bf16[128,2048]{1,0:T(8,128)(2,1)S(1)} %bitcast.78, f32[128,4096]{1,0:T(8,128)S(1)} %copy-done.7, s32[4096]{0:T(1024)S(1)} %fusion.95, f32[128]{0:T(128)S(1)} %get-tuple-element.10, s32[128]{0:T(128)S(1)} %eq.17), kind=kOutput, calls=%fused_computation | convolution fusion | flops 1076887552 | bytes 19153920 | tf_op jit(solution)/shard_map/dot_general | solution.py:120
  207.2 33.3 %copy.33 = f32[4096,2048]{1,0:T(8,128)} copy(f32[4096,2048]{0,1:T(8,128)} %convolution_dynamic-update-slice_fusion) | data formatting | bytes 67108864 | tf_op jit(solution)/shard_map/concatenate | solution.py:130
  240.6 23.0 %copy.34 = f32[2,32,64,2048]{3,2,1,0:T(8,128)} copy(f32[2,32,64,2048]{3,2,0,1:T(8,128)} %bitcast.60) | data formatting | bytes 67108864 | tf_op jit(solution)/shard_map/transpose | solution.py:74
  263.9 41.7 %reduce-scatter.3.cloned.1.call-done = f32[32,64,2048]{2,1,0:T(8,128)} async-done(((f32[64,64,2048]{2,1,0:T(8,128)}), f32[32,64,2048]{2,1,0:T(8,128)}) %reduce-scatter.3.cloned.1.call-update) | async-done | bytes 16777232 | tf_op jit(solution)/shard_map/reduce_scatter | solution.py:75
  305.7 2.1 fusion.50
  307.8 1.8 fusion.47
  309.7 1.8 fusion.44
  311.5 1.8 fusion.41
  313.4 2.4 fusion.38
  315.8 2.3 fusion.35
  318.1 2.4 fusion.31
  320.5 2.9 fusion.10
  323.4 4.9 fusion
  328.7 181.0 %all_to_all.21 = f32[2,64,2048]{2,1,0:T(8,128)S(1)} all-to-all(f32[2,64,2048]{2,1,0:T(8,128)S(1)} %bitcast.79), channel_id=1, replica_groups=mesh['dp_0'=4,'dp_1'=2,'dp_2'=4,'dp_3'=2,'rep'=2] {'rep'}, dimensions={0} | all-to-all | bytes 2097152 | tf_op jit(solution)/shard_map/all_to_all | solution.py:66
  509.6 0.9 reduce_sum.99
  510.5 4.3 reduce-scatter.5.cloned.1.call-done
  (81 shorter events, 4.9 us)
Async XLA Ops:
  7.2 17.3 %copy-start.30 = (s32[64]{0:T(128)S(1)}, s32[64]{0:T(128)}, u32[]{:S(2)}) copy-start(s32[64]{0:T(128)} %param.5) | copy-start | bytes 772
  7.2 126.6 %all-gather.2.cloned.1.call-start = ((), (), s32[]{:S(2)}) async-start(), calls=%async_computation.6 | async-start | bytes 17039360 | tf_op jit(solution)/shard_map/all_gather | solution.py:148
  9.7 14.7 %all-to-all-start = ((bf16[2,64,2048]{2,1,0:T(8,128)(2,1)}), bf16[2,64,2048]{2,1,0:T(8,128)(2,1)S(1)}, u32[]{:S(2)}, u32[]{:S(2)}) async-start(bf16[2,64,2048]{2,1,0:T(8,128)(2,1)} %broadcast_in_dim.10), calls=%async_computation | async-start | bytes 1048576 | tf_op jit(solution)/shard_map/all_to_all | solution.py:21
  24.4 111.5 %copy-start.11 = (bf16[2,64,2048]{2,1,0:T(8,128)(2,1)}, bf16[2,64,2048]{2,1,0:T(8,128)(2,1)S(1)}, u32[]{:S(2)}) copy-start(bf16[2,64,2048]{2,1,0:T(8,128)(2,1)S(1)} %all-to-all-done) | copy-start | bytes 1572868
  25.0 139.1 %all-to-all-start.2 = ((s32[2,1,64]{2,1,0:T(1,128)}), s32[2,1,64]{2,1,0:T(1,128)S(1)}, u32[]{:S(2)}, u32[]{:S(2)}) async-start(s32[2,1,64]{2,1,0:T(1,128)} %broadcast_in_dim.12), calls=%async_computation.2 | async-start | bytes 2048 | tf_op jit(solution)/shard_map/all_to_all | solution.py:21
  135.5 2.6 copy-start
  138.1 2.6 copy-start.1
  140.7 2.6 copy-start.2
  143.4 2.6 copy-start.3
  146.0 2.5 copy-start.4
  151.5 4.6 copy-start.5
  156.1 6.2 %copy-start.8 = (f32[128,4096]{1,0:T(8,128)}, f32[128,4096]{1,0:T(8,128)S(1)}, u32[]{:S(2)}) copy-start(f32[128,4096]{1,0:T(8,128)S(1)} %get-tuple-element.34) | copy-start | bytes 6291460
  162.3 1.4 copy-start.6
  164.7 9.9 %all-to-all-start.1 = ((f32[2,18,128]{2,1,0:T(8,128)}), f32[2,18,128]{2,1,0:T(8,128)S(1)}, u32[]{:S(2)}, u32[]{:S(2)}) async-start(f32[2,18,128]{2,1,0:T(8,128)} %broadcast_in_dim.11), calls=%async_computation.1 | async-start | bytes 49152 | tf_op jit(solution)/shard_map/all_to_all | solution.py:21
  169.2 136.4 %reduce-scatter.3.cloned.1.call-start = ((), (), s32[]{:S(2)}) async-start(), calls=%async_computation.7 | async-start | bytes 50331648 | tf_op jit(solution)/shard_map/reduce_scatter | solution.py:75
  170.4 28.6 %copy-start.28 = (s32[128]{0:T(128)}, s32[128]{0:T(128)S(1)}, u32[]{:S(2)}) copy-start(s32[128]{0:T(128)S(1)} %eq.17) | copy-start | bytes 1540
  174.7 24.3 %copy-start.26 = (f32[128]{0:T(128)}, f32[128]{0:T(128)S(1)}, u32[]{:S(2)}) copy-start(f32[128]{0:T(128)S(1)} %get-tuple-element.10) | copy-start | bytes 1540
  174.7 8.7 %copy-start.12 = (bf16[2,64,2048]{2,1,0:T(8,128)(2,1)S(1)}, bf16[2,64,2048]{2,1,0:T(8,128)(2,1)}, u32[]{:S(2)}) copy-start(bf16[2,64,2048]{2,1,0:T(8,128)(2,1)} %copy-done.11) | copy-start | bytes 1572868
  183.3 5.2 copy-start.17
  183.3 5.2 copy-start.19
  183.4 5.2 copy-start.15
  183.4 6.6 %copy-start.13 = (bf16[128,4096]{1,0:T(8,128)(2,1)}, bf16[128,4096]{1,0:T(8,128)(2,1)S(1)}, u32[]{:S(2)}) copy-start(bf16[128,4096]{1,0:T(8,128)(2,1)S(1)} %get-tuple-element.7) | copy-start | bytes 3145732
  183.4 11.1 %copy-start.21 = (bf16[128,4096]{1,0:T(8,128)(2,1)}, bf16[128,4096]{1,0:T(8,128)(2,1)S(1)}, u32[]{:S(2)}) copy-start(bf16[128,4096]{1,0:T(8,128)(2,1)S(1)} %get-tuple-element.3) | copy-start | bytes 3145732
  183.4 11.1 %copy-start.23 = (bf16[128,4096]{1,0:T(8,128)(2,1)}, bf16[128,4096]{1,0:T(8,128)(2,1)S(1)}, u32[]{:S(2)}) copy-start(bf16[128,4096]{1,0:T(8,128)(2,1)S(1)} %get-tuple-element.2) | copy-start | bytes 3145732
  183.4 11.1 %copy-start.9 = (bf16[128,4096]{1,0:T(8,128)(2,1)}, bf16[128,4096]{1,0:T(8,128)(2,1)S(1)}, u32[]{:S(2)}) copy-start(bf16[128,4096]{1,0:T(8,128)(2,1)S(1)} %get-tuple-element.9) | copy-start | bytes 3145732
  194.5 4.5 copy-start.7
  263.6 251.2 %reduce-scatter.5.cloned.1.call-start = ((), (), s32[]{:S(2)}) async-start(), calls=%async_computation.8 | async-start | bytes 17301504 | tf_op jit(solution)/shard_map/reduce_scatter | solution.py:76
  305.6 2.1 copy-start.22
  305.6 4.0 copy-start.20
  307.8 3.7 copy-start.18
  309.6 3.7 copy-start.16
  311.5 4.3 copy-start.14
  318.1 2.4 copy-start.10
  320.4 2.9 copy-start.27
  320.4 2.9 copy-start.29
  323.4 4.9 copy-start.24
  323.4 4.9 copy-start.25
Sparse Core Ops, SparseCore 0:
  9.7 123.9 all-gather.1
  263.7 41.8 reduce-scatter.2
  308.6 206.1 reduce-scatter.4
where the time goes:
time: 523 us; the launch traced here: 521 us
  blocking collectives  181 us (35%)
  waiting for transfers between devices  166 us (32%)
  matrix products  70.7 us (14%)
  local copies, waits for them, and re-layouts  61.9 us (12%)
  other arithmetic  14.5 us (3%)
  between operations  14.2 us (3%)
  starting transfers between devices  13.2 us (3%)
    all_to_all x1, blocking collectives, sum_at_owner(): lax.all_to_all(blocks, axis, split_axis=0, concat_axis=0, tiled=True)  181 us
    all_gather x1, waiting for transfers between devices, on_device(): partner_docs = lax.all_gather(documents, DP, axis=0, tiled=True)  105 us
    reduce_scatter x1, waiting for transfers between devices, sum_by_chip(): blocks = lax.psum_scatter(blocks, core, scatter_dimension=0, tiled=True)  41.7 us
    concatenate x2, local copies, waits for them, and re-layouts, spread(): return jnp.concatenate(pieces, axis=1)  33.7 us
    dot_general x9, matrix products, contract(): lax.dot_general(first_op, second_op, (((1,), (1,)), ((), ())), preferred_...  24.4 us
    dot_general x9, matrix products, spread(): lax.dot_general(bands[nested], block_part, (((0,), (0,)), ((), ())), pref...  23.8 us
    transpose x1, local copies, waits for them, and re-layouts, sum_by_chip(): blocks = blocks.reshape(*sizes, *inside).swapaxes(0, 1).reshape(-1, *inside)  23 us
    dot_general x9, matrix products, spread(): jnp.dot(bands[nested], block_part, preferred_element_type=jnp.float32)  22.4 us
  transfers between devices with their start and end apart: 6, of which 5 were waited for; matrix products, arithmetic and copies ran while one was open for 11% of the time, Pallas kernels for 0%

commit v1 on v0

--- a/solution.py
+++ b/solution.py
@@ -145,7 +145,10 @@
     rep_index = lax.axis_index("rep")
     rep_count = lax.axis_size("rep")
     pair_rows, pair_partner = (collect(queries, "rep", 0), collect(partner, "rep", 0))
-    partner_docs = lax.all_gather(documents, DP, axis=0, tiled=True)
+    count = lax.axis_size(DP)
+    parts = jnp.stack([documents for _ in range(count)])
+    parts = lax.all_to_all(parts, DP, split_axis=0, concat_axis=0)
+    partner_docs = jnp.concatenate(parts, axis=0)
     col_pos = jnp.arange(partner_docs.shape[0], dtype=jnp.int32)
     col_ids = (col_pos // own_rows * rep_count + rep_index) * own_rows + col_pos % own_rows
     target = (pair_partner[:, None] == col_ids[None, :]).astype(jnp.float32)

time: 523 us -> 661 us (1.26)
  waiting for transfers between devices: 166 us -> 280 us
  blocking collectives: 181 us -> 196 us
    all_to_all x0 -> x1, waiting for transfers between devices: none -> 218 us  [on_device(): parts = lax.all_to_all(parts, DP, split_axis=0, concat_axis=0)]
    all_gather x1 -> x0, waiting for transfers between devices: 105 us -> none  [on_device(): partner_docs = lax.all_gather(documents, DP, axis=0, tiled=True)]
    all_to_all x0 -> x1, blocking collectives: none -> 14.5 us  [copy_for_each(): return lax.all_to_all(copies, axis, split_axis=0, concat_axis=0, tiled=True)]
    reduce_scatter x1, waiting for transfers between devices: 41.7 us -> 52.8 us  [sum_by_chip(): blocks = lax.psum_scatter(blocks, core, scatter_dimension=0, tiled=True)]
    all_to_all x3 -> x2, waiting for transfers between devices: 13.7 us -> 4.22 us  [copy_for_each(): return lax.all_to_all(copies, axis, split_axis=0, concat_axis=0, tiled=True)]
    all_to_all x0 -> x1, starting transfers between devices: none -> 8.79 us  [on_device(): parts = lax.all_to_all(parts, DP, split_axis=0, concat_axis=0)]
    another operation x0 -> x1, local copies, waits for them, and re-layouts: none -> 6.68 us  [on_device(): parts = jnp.stack([documents for _ in range(count)])]
  transfers between devices with their start and end apart: 6 -> 5, of which waited for: 5 -> 4; matrix products, arithmetic and copies ran while one was open for 11% -> 8% of each run, Pallas kernels for 0% -> 0%
where the time goes in v1:
time: 661 us; the launch traced here: 660 us
  waiting for transfers between devices  280 us (42%)
  blocking collectives  196 us (30%)
  matrix products  71.2 us (11%)
  local copies, waits for them, and re-layouts  66.8 us (10%)
  starting transfers between devices  17 us (3%)
  other arithmetic  14.5 us (2%)
  between operations  14.5 us (2%)
    all_to_all x1, waiting for transfers between devices, on_device(): parts = lax.all_to_all(parts, DP, split_axis=0, concat_axis=0)  218 us
    all_to_all x1, blocking collectives, sum_at_owner(): lax.all_to_all(blocks, axis, split_axis=0, concat_axis=0, tiled=True)  181 us
    reduce_scatter x1, waiting for transfers between devices, sum_by_chip(): blocks = lax.psum_scatter(blocks, core, scatter_dimension=0, tiled=True)  52.8 us
    concatenate x2, local copies, waits for them, and re-layouts, spread(): return jnp.concatenate(pieces, axis=1)  33.7 us
    dot_general x9, matrix products, contract(): lax.dot_general(first_op, second_op, (((1,), (1,)), ((), ())), preferred_...  24.9 us
    dot_general x9, matrix products, spread(): lax.dot_general(bands[nested], block_part, (((0,), (0,)), ((), ())), pref...  23.8 us
    transpose x1, local copies, waits for them, and re-layouts, sum_by_chip(): blocks = blocks.reshape(*sizes, *inside).swapaxes(0, 1).reshape(-1, *inside)  23 us
    dot_general x9, matrix products, spread(): jnp.dot(bands[nested], block_part, preferred_element_type=jnp.float32)  22.4 us
  transfers between devices with their start and end apart: 5, of which 4 were waited for; matrix products, arithmetic and copies ran while one was open for 8% of the time, Pallas kernels for 0%

profile of v1, /device:TPU:0, one launch (start us, length us, event | category | flops | bytes accessed | tf_op | source)
XLA Modules:
  0.0 659.7 jit_solution(3719807217325395127)
XLA Ops:
  7.2 1.0 broadcast_in_dim.10
  8.2 14.5 %all_to_all.26 = bf16[2,64,2048]{2,1,0:T(8,128)(2,1)S(1)} all-to-all(bf16[2,64,2048]{2,1,0:T(8,128)(2,1)S(1)} %broadcast_in_dim.10), channel_id=1, replica_groups=mesh['dp_0'=4,'dp_1'=2,'dp_2'=4,'dp_3'=2,'rep'=2] {'rep'}, dimensions={0} | all-to-all | bytes 1048576 | tf_op jit(solution)/shard_map/all_to_all | solution.py:21
  22.7 6.7 %stack.38 = bf16[64,64,2048]{2,1,0:T(8,128)(2,1)} broadcast(bf16[64,2048]{1,0:T(8,128)(2,1)} %param.4), dimensions={1,2} | broadcast | bytes 17039360 | tf_op jit(solution)/shard_map/stack | solution.py:149
  29.4 8.8 %all-to-all-start.1 = ((bf16[64,64,2048]{2,1,0:T(8,128)(2,1)}), bf16[64,64,2048]{2,1,0:T(8,128)(2,1)}, u32[]{:S(2)}, u32[]{:S(2)}) async-start(bf16[64,64,2048]{2,1,0:T(8,128)(2,1)} %stack.38), calls=%async_computation.1 | async-start | bytes 33554432 | tf_op jit(solution)/shard_map/all_to_all | solution.py:150
  38.2 218.2 %all-to-all-done.1 = bf16[64,64,2048]{2,1,0:T(8,128)(2,1)} async-done(((bf16[64,64,2048]{2,1,0:T(8,128)(2,1)}), bf16[64,64,2048]{2,1,0:T(8,128)(2,1)}, u32[]{:S(2)}, u32[]{:S(2)}) %all-to-all-start.1) | async-done | bytes 16777248 | tf_op jit(solution)/shard_map/all_to_all | solution.py:150
  256.3 0.6 broadcast_in_dim.12
  256.9 3.2 all-to-all-start.3
  260.1 1.7 multiply_reduce_fusion.7
  261.9 2.6 multiply_reduce_fusion.6
  264.5 0.5 exponential_reduce_fusion.8
  265.0 2.1 multiply_reduce_fusion.5
  267.6 2.1 multiply_reduce_fusion.4
  269.8 0.5 exponential_reduce_fusion.6
  270.3 2.1 multiply_reduce_fusion.3
  272.9 2.0 multiply_reduce_fusion.2
  275.4 2.5 multiply_reduce_fusion.1
  278.4 4.1 multiply_reduce_fusion
  283.0 5.7 fusion.110
  290.1 0.6 broadcast_in_dim.11
  290.7 4.8 all-to-all-start.2
  295.5 0.5 broadcast.144
  296.0 0.6 reduce.3
  296.7 4.2 all-to-all-done.2
  300.9 8.6 %fusion.30 = (bf16[128,4096]{1,0:T(8,128)(2,1)S(1)}, bf16[128,4096]{1,0:T(8,128)(2,1)S(1)}, bf16[128,4096]{1,0:T(8,128)(2,1)S(1)}, bf16[128,4096]{1,0:T(8,128)(2...) fusion(f32[128,4096]{1,0:T(8,128)} %copy-done, ...), kind=kLoop, calls=%fused_computation.51 | loop fusion | flops 27787264 | bytes 27284480 | tf_op jit(solution)/shard_map/convert_element_type | solution.py:110
  309.6 1.3 convolution_dynamic-update-slice_fusion.8
  310.9 1.6 convolution_dynamic-update-slice_fusion.7
  312.5 1.1 convolution_dynamic-update-slice_fusion.6
  313.6 1.2 convolution_dynamic-update-slice_fusion.5
  314.8 1.4 convolution_dynamic-update-slice_fusion.4
  316.2 1.8 convolution_dynamic-update-slice_fusion.3
  318.0 2.7 convolution_dynamic-update-slice_fusion.2
  320.7 4.5 convolution_dynamic-update-slice_fusion.1
  325.2 8.2 %convolution_dynamic-update-slice_fusion = f32[4096,2048]{0,1:T(8,128)} fusion(f32[4096,2048]{0,1:T(8,128)} %convolution_dynamic-update-slice_fusion.1, bf16[128,2048]{1,0:T(8,128)(2,1)S(1)} %bitcast.79, f32[128,4096]{1,0:T(8,128)S(1)} %copy-done.7, s32[4096]{0:T(1024)S(1)} %fusion.95, f32[128]{0:T(128)S(1)} %get-tuple-element.10, s32[128]{0:T(128)S(1)} %eq.17), kind=kOutput, calls=%fused_computation | convolution fusion | flops 1076887552 | bytes 19153920 | tf_op jit(solution)/shard_map/dot_general | solution.py:120
  333.5 33.3 %copy.33 = f32[4096,2048]{1,0:T(8,128)} copy(f32[4096,2048]{0,1:T(8,128)} %convolution_dynamic-update-slice_fusion) | data formatting | bytes 67108864 | tf_op jit(solution)/shard_map/concatenate | solution.py:130
  366.8 23.0 %copy.34 = f32[2,32,64,2048]{3,2,1,0:T(8,128)} copy(f32[2,32,64,2048]{3,2,0,1:T(8,128)} %bitcast.61) | data formatting | bytes 67108864 | tf_op jit(solution)/shard_map/transpose | solution.py:74
  390.1 52.8 %reduce-scatter.3.cloned.1.call-done = f32[32,64,2048]{2,1,0:T(8,128)} async-done(((f32[64,64,2048]{2,1,0:T(8,128)}), f32[32,64,2048]{2,1,0:T(8,128)}) %reduce-scatter.3.cloned.1.call-update) | async-done | bytes 16777232 | tf_op jit(solution)/shard_map/reduce_scatter | solution.py:75
  443.0 2.1 fusion.50
  445.1 1.8 fusion.47
  447.0 1.8 fusion.44
  448.9 1.8 fusion.41
  450.7 2.4 fusion.38
  453.1 2.3 fusion.35
  455.4 2.4 fusion.31
  457.8 2.9 fusion.10
  460.7 4.9 fusion
  466.0 181.0 %all_to_all.27 = f32[2,64,2048]{2,1,0:T(8,128)S(1)} all-to-all(f32[2,64,2048]{2,1,0:T(8,128)S(1)} %bitcast.80), channel_id=1, replica_groups=mesh['dp_0'=4,'dp_1'=2,'dp_2'=4,'dp_3'=2,'rep'=2] {'rep'}, dimensions={0} | all-to-all | bytes 2097152 | tf_op jit(solution)/shard_map/all_to_all | solution.py:66
  647.0 0.9 reduce_sum.99
  647.9 5.0 reduce-scatter.5.cloned.1.call-done
  (80 shorter events, 4.8 us)
Async XLA Ops:
  22.7 239.2 %copy-start.11 = (bf16[2,64,2048]{2,1,0:T(8,128)(2,1)}, bf16[2,64,2048]{2,1,0:T(8,128)(2,1)S(1)}, u32[]{:S(2)}) copy-start(bf16[2,64,2048]{2,1,0:T(8,128)(2,1)S(1)} %all_to_all.26) | copy-start | bytes 1572868
  29.4 227.0 %copy-start.30 = (s32[64]{0:T(128)S(1)}, s32[64]{0:T(128)}, u32[]{:S(2)}) copy-start(s32[64]{0:T(128)} %param.5) | copy-start | bytes 772
  29.4 227.0 %all-to-all-start.1 = ((bf16[64,64,2048]{2,1,0:T(8,128)(2,1)}), bf16[64,64,2048]{2,1,0:T(8,128)(2,1)}, u32[]{:S(2)}, u32[]{:S(2)}) async-start(bf16[64,64,2048]{2,1,0:T(8,128)(2,1)} %stack.38), calls=%async_computation.1 | async-start | bytes 33554432 | tf_op jit(solution)/shard_map/all_to_all | solution.py:150
  256.9 33.2 %all-to-all-start.3 = ((s32[2,1,64]{2,1,0:T(1,128)}), s32[2,1,64]{2,1,0:T(1,128)S(1)}, u32[]{:S(2)}, u32[]{:S(2)}) async-start(s32[2,1,64]{2,1,0:T(1,128)} %broadcast_in_dim.12), calls=%async_computation.3 | async-start | bytes 2048 | tf_op jit(solution)/shard_map/all_to_all | solution.py:21
  261.9 2.7 copy-start
  264.5 2.6 copy-start.1
  267.1 2.6 copy-start.2
  269.7 2.6 copy-start.3
  272.4 2.5 copy-start.4
  277.9 4.6 copy-start.5
  282.5 6.2 copy-start.8
  288.6 1.4 copy-start.6
  290.7 10.2 %all-to-all-start.2 = ((f32[2,18,128]{2,1,0:T(8,128)}), f32[2,18,128]{2,1,0:T(8,128)S(1)}, u32[]{:S(2)}, u32[]{:S(2)}) async-start(f32[2,18,128]{2,1,0:T(8,128)} %broadcast_in_dim.11), calls=%async_computation.2 | async-start | bytes 49152 | tf_op jit(solution)/shard_map/all_to_all | solution.py:21
  295.5 147.5 %reduce-scatter.3.cloned.1.call-start = ((), (), s32[]{:S(2)}) async-start(), calls=%async_computation.7 | async-start | bytes 50331648 | tf_op jit(solution)/shard_map/reduce_scatter | solution.py:75
  296.7 28.6 %copy-start.28 = (s32[128]{0:T(128)}, s32[128]{0:T(128)S(1)}, u32[]{:S(2)}) copy-start(s32[128]{0:T(128)S(1)} %eq.17) | copy-start | bytes 1540
  300.9 24.3 %copy-start.26 = (f32[128]{0:T(128)}, f32[128]{0:T(128)S(1)}, u32[]{:S(2)}) copy-start(f32[128]{0:T(128)S(1)} %get-tuple-element.10) | copy-start | bytes 1540
  300.9 8.7 %copy-start.12 = (bf16[2,64,2048]{2,1,0:T(8,128)(2,1)S(1)}, bf16[2,64,2048]{2,1,0:T(8,128)(2,1)}, u32[]{:S(2)}) copy-start(bf16[2,64,2048]{2,1,0:T(8,128)(2,1)} %copy-done.11) | copy-start | bytes 1572868
  309.6 5.2 copy-start.17
  309.6 5.2 copy-start.19
  309.6 5.2 copy-start.15
  309.6 6.6 %copy-start.13 = (bf16[128,4096]{1,0:T(8,128)(2,1)}, bf16[128,4096]{1,0:T(8,128)(2,1)S(1)}, u32[]{:S(2)}) copy-start(bf16[128,4096]{1,0:T(8,128)(2,1)S(1)} %get-tuple-element.7) | copy-start | bytes 3145732
  309.6 11.1 %copy-start.21 = (bf16[128,4096]{1,0:T(8,128)(2,1)}, bf16[128,4096]{1,0:T(8,128)(2,1)S(1)}, u32[]{:S(2)}) copy-start(bf16[128,4096]{1,0:T(8,128)(2,1)S(1)} %get-tuple-element.3) | copy-start | bytes 3145732
  309.6 11.1 %copy-start.23 = (bf16[128,4096]{1,0:T(8,128)(2,1)}, bf16[128,4096]{1,0:T(8,128)(2,1)S(1)}, u32[]{:S(2)}) copy-start(bf16[128,4096]{1,0:T(8,128)(2,1)S(1)} %get-tuple-element.2) | copy-start | bytes 3145732
  309.6 11.1 %copy-start.9 = (bf16[128,4096]{1,0:T(8,128)(2,1)}, bf16[128,4096]{1,0:T(8,128)(2,1)S(1)}, u32[]{:S(2)}) copy-start(bf16[128,4096]{1,0:T(8,128)(2,1)S(1)} %get-tuple-element.9) | copy-start | bytes 3145732
  320.7 4.5 copy-start.7
  389.8 263.0 %reduce-scatter.5.cloned.1.call-start = ((), (), s32[]{:S(2)}) async-start(), calls=%async_computation.8 | async-start | bytes 17301504 | tf_op jit(solution)/shard_map/reduce_scatter | solution.py:76
  443.0 2.1 copy-start.22
  443.0 4.0 copy-start.20
  445.1 3.7 copy-start.18
  447.0 3.7 copy-start.16
  448.9 4.3 copy-start.14
  455.4 2.4 copy-start.10
  457.8 2.9 copy-start.27
  457.8 2.9 copy-start.29
  460.7 4.9 copy-start.24
  460.7 4.9 copy-start.25
Sparse Core Ops, SparseCore 0:
  390.0 52.9 reduce-scatter.2
  445.9 206.8 reduce-scatter.4
